TPU v7x, 32 devices: a whole 2x2x4 slice. The times are simulated.
32 devices in a mesh: grp: 8 (over z, y), slab: 4 (over x, core).
Axes of the slice: x: 2, y: 2, z: 4, core: 2. Of those that a mesh axis runs over, the one named last changes fastest.
Arguments:
- grids: float32 [8, 512, 4096], P('grp', 'slab'), may hold values from -6 to 6
- first_level: int32 [8], P('grp'), may hold values from 6 to 8, as said below
- coeffs: int32 [8], P('grp'), may hold values from -3 to 3
- slot_map: int32 [8, 512], P('grp', 'slab'), may hold values from 0 to 1023, as said below
Outputs:
- combined_grid: float32 [8, 512, 4096], P('grp', 'slab')
Inputs may be any that keep to these rules, and one draw needn't show every extreme that they name: The second dimension of grid g has level 9 minus first_level[g]. Every value of the range is taken by some grid. `slot_map`: grid g's point with first coordinate i of 2^a points lies at position i / 2^a of a periodic unit interval, and likewise in the second dimension. Two rows of any grids at the same position in the first two dimensions share a slot; rows of one grid have distinct slots; every slot is used by some grid. The rows held by the s-th index of slab (first coordinates in the s-th of 4 equal ranges) of every grid have slots in the s-th of 4 equal aligned ranges of the 1024 slots.
All inputs are finite; a program needn't handle non-finite values.
Results may differ from a plain program's by a relative error of at most 0.0003.
Values sent between devices are 32-bit elements; how exact they have to be, the bound alone decides.
A program may use at most 64 MiB of HBM per device.

v0:
```python
import jax
import jax.numpy as jnp
from jax import lax
from jax.sharding import PartitionSpec as P

P2 = 16
P3 = 16
P4 = 16
LEVEL_SUM = 9
PLANE = 8
ROWS = 512


def hier_weight(target, source, period):
    spread = target & -target
    interior = (target != 0).astype(jnp.float32)
    left_side = (source == target - spread).astype(jnp.float32)
    right_side = (source == (target + spread) % period).astype(jnp.float32)
    return (target == source).astype(jnp.float32) - 0.5 * interior * (left_side + right_side)


def dehier_weight(target, source, period):
    spread = jnp.maximum(source & -source, 1).astype(jnp.float32)
    apart = jnp.abs(target - source)
    apart = jnp.minimum(apart, period - apart).astype(jnp.float32)
    return jnp.where(source == 0, 1.0, jnp.maximum(0.0, 1.0 - apart / spread))


def square_table(maker, length):
    points = jnp.arange(length, dtype=jnp.int32)
    return maker(points[:, None], points[None, :], length)


def inner_apply(values, third_op, rest_op):
    count = values.shape[0]
    shaped = values.reshape(count, P2, P3 * P4)
    shaped = jnp.einsum("ij,rjk->rik", third_op, shaped, precision=lax.Precision.HIGHEST)
    shaped = jnp.einsum("rjk,lk->rjl", shaped, rest_op, precision=lax.Precision.HIGHEST)
    return shaped.reshape(count, P2 * P3 * P4)


def exact_dot(left, right):
    return jnp.dot(left, right, precision=lax.Precision.HIGHEST, preferred_element_type=jnp.float32)


def shards(grids, first_level, coeffs, slot_map):
    grid_rows = grids[0]
    level = first_level[0]
    second = LEVEL_SUM - level
    rows_dev = grid_rows.shape[0]
    width = grid_rows.shape[1]
    slabs = lax.axis_size("slab")
    slab_index = lax.axis_index("slab")
    span = rows_dev >> second
    row_ids = jnp.arange(rows_dev, dtype=jnp.int32)
    first_pos = row_ids >> second
    second_pos = row_ids & (1 << second) - 1
    slab_ids = jnp.arange(slabs, dtype=jnp.int32)
    same_first = (first_pos[:, None] == first_pos[None, :]).astype(jnp.float32)
    hier_third = square_table(hier_weight, P2)
    hier_rest = jnp.kron(square_table(hier_weight, P3), square_table(hier_weight, P4))
    values = inner_apply(grid_rows, hier_third, hier_rest)
    second_op = same_first * hier_weight(second_pos[:, None], second_pos[None, :], 1 << second)
    values = exact_dot(second_op, values)
    plane = values[:PLANE]
    planes = lax.all_gather(plane[None], "slab", axis=0, tiled=True)
    following = lax.dynamic_index_in_dim(planes, (slab_index + 1) % slabs, 0, keepdims=False)
    extended = jnp.concatenate([values, following], axis=0)
    ext_ids = jnp.arange(rows_dev + PLANE, dtype=jnp.int32)
    ext_first = ext_ids >> second
    ext_second = ext_ids & (1 << second) - 1
    spread = first_pos & -first_pos
    interior = (first_pos != 0).astype(jnp.float32)[:, None]
    same_second = (second_pos[:, None] == ext_second[None, :]).astype(jnp.float32)
    centre = (ext_first[None, :] == first_pos[:, None]).astype(jnp.float32)
    below = (ext_first[None, :] == (first_pos - spread)[:, None]).astype(jnp.float32)
    above = (ext_first[None, :] == (first_pos + spread)[:, None]).astype(jnp.float32)
    fine_op = same_second * (centre - 0.5 * interior * (below + above))
    surplus = exact_dot(fine_op, extended)
    coarse_weights = hier_weight(slab_index, slab_ids, slabs)
    coarse = jnp.einsum("q,qpk->pk", coarse_weights, planes, precision=lax.Precision.HIGHEST)
    padded = jnp.concatenate([coarse, jnp.zeros((rows_dev - PLANE, width), jnp.float32)], axis=0)
    surplus = jnp.where((first_pos == 0)[:, None], padded, surplus)
    scaled = coeffs[0].astype(jnp.float32) * surplus
    per_slab = 2 * ROWS // slabs
    slot_local = slot_map[0] % per_slab
    slot_ids = jnp.arange(per_slab, dtype=jnp.int32)
    gather_op = (slot_local[None, :] == slot_ids[:, None]).astype(jnp.float32)
    term = exact_dot(gather_op, scaled)
    total = lax.psum(term, "grp")
    spread_op = (slot_local[:, None] == slot_ids[None, :]).astype(jnp.float32)
    combined = exact_dot(spread_op, total)
    back_third = square_table(dehier_weight, P2)
    back_rest = jnp.kron(square_table(dehier_weight, P3), square_table(dehier_weight, P4))
    values = inner_apply(combined, back_third, back_rest)
    back_second = same_first * dehier_weight(second_pos[:, None], second_pos[None, :], 1 << second)
    values = exact_dot(back_second, values)
    top_plane = values[:PLANE]
    top_planes = lax.all_gather(top_plane[None], "slab", axis=0, tiled=True)
    here_weights = dehier_weight(slab_index, slab_ids, slabs)
    there_weights = dehier_weight((slab_index + 1) % slabs, slab_ids, slabs)
    here = jnp.einsum("q,qpk->pk", here_weights, top_planes, precision=lax.Precision.HIGHEST)
    there = jnp.einsum("q,qpk->pk", there_weights, top_planes, precision=lax.Precision.HIGHEST)
    same_row_second = (second_pos[:, None] == second_pos[None, :]).astype(jnp.float32)
    inside = (first_pos[None, :] != 0).astype(jnp.float32)
    local_op = (
        same_row_second * inside * dehier_weight(first_pos[:, None], first_pos[None, :], 2 * span)
    )
    fraction = first_pos.astype(jnp.float32) / span.astype(jnp.float32)
    plane_ids = jnp.arange(PLANE, dtype=jnp.int32)
    plane_pick = (second_pos[:, None] == plane_ids[None, :]).astype(jnp.float32)
    nodal = exact_dot(local_op, values)
    nodal = nodal + exact_dot((1.0 - fraction)[:, None] * plane_pick, here)
    nodal = nodal + exact_dot(fraction[:, None] * plane_pick, there)
    return nodal[None]


def solution(mesh):
    in_specs = (P("grp", "slab", None), P("grp"), P("grp"), P("grp", "slab"))
    out_specs = P("grp", "slab", None)
    return jax.shard_map(shards, mesh=mesh, in_specs=in_specs, out_specs=out_specs, check_vma=False)
```

profile of v0, /device:TPU:0, one launch (start us, length us, event | category | flops | bytes accessed | tf_op | source)
XLA Modules:
  0.0 230.8 jit_solution(8167477807761341772)
XLA Ops:
  7.5 2.3 copy.16
  9.8 1.9 fusion.114
  11.8 1.5 broadcast_multiply_fusion.1
  13.3 2.4 %reshape.448 = f32[256,256,1]{1,0,2:T(8,128)S(1)} reshape(f32[16,16,16,16]{3,2,1,0:T(8,128)} %broadcast_multiply_fusion.1) | data formatting | bytes 524288 | tf_op jit(solution)/shard_map/jit(kron)/mul | solution.py:61
  15.7 3.2 %fusion.7 = f32[128,16,256]{0,2,1:T(8,128)S(1)} fusion(f32[256,256,1]{1,0,2:T(8,128)S(1)} %reshape.448, f32[16,128,256]{2,0,1:T(8,128)S(1)} %fusion.114), kind=kOutput, calls=%fused_computation.10 | convolution fusion | flops 1610612736 | bytes 4456448 | tf_op jit(solution)/shard_map/rjk,lk->rjl/dot_general | solution.py:38
  19.0 2.0 fusion.39
  21.0 8.8 %all-gather = f32[32,4096]{1,0:T(8,128)S(1)} all-gather(f32[8,4096]{1,0:T(8,128)S(1)} %slice.8), channel_id=2, replica_groups=mesh['grp'=8,'slab'=4] {'slab'}, dimensions={0}, use_global_device_ids=true | all-gather | bytes 655360 | tf_op jit(solution)/shard_map/all_gather | solution.py:66
  29.8 1.2 fusion.11
  31.8 2.1 fusion.1
  33.9 3.9 %fusion.29 = f32[256,4096]{1,0:T(8,128)} fusion(f32[128,4096]{1,0:T(8,128)S(1)} %fusion.1, s32[128]{0:T(128)S(1)} %fusion.130), kind=kOutput, calls=%fused_computation.38 | convolution fusion | flops 1610645504 | bytes 6291968 | tf_op jit(solution)/shard_map/dot_general | solution.py:43
  37.9 0.2 broadcast_multiply_fusion
  38.1 0.9 reshape.452
  39.1 156.1 %all-reduce.3.cloned.1.call-done = f32[256,4096]{1,0:T(8,128)} async-done(((f32[256,4096]{1,0:T(8,128)}), f32[256,4096]{1,0:T(8,128)}) %all-reduce.3.cloned.1.call-update) | async-done | bytes 4194320 | tf_op jit(solution)/shard_map/psum | solution.py:90
  195.2 3.9 %fusion.28 = f32[128,4096]{1,0:T(8,128)S(1)} fusion(f32[256,4096]{1,0:T(8,128)} %all-reduce.3.cloned.1.call-done, s32[128]{0:T(128)S(1)} %and_select_fusion.3), kind=kOutput, calls=%fused_computation.37 | convolution fusion | flops 1610645504 | bytes 6291968 | tf_op jit(solution)/shard_map/dot_general | solution.py:43
  199.1 0.7 copy.17
  199.8 1.9 fusion.112
  201.7 3.5 %fusion.5 = f32[128,16,256]{0,2,1:T(8,128)S(1)} fusion(f32[256,256,1]{1,0,2:T(8,128)S(1)} %reshape.452, f32[128,256,16]{1,2,0:T(8,128)S(1)} %fusion.112), kind=kOutput, calls=%fused_computation.8 | convolution fusion | flops 1610612736 | bytes 4456448 | tf_op jit(solution)/shard_map/rjk,lk->rjl/dot_general | solution.py:38
  205.2 2.0 fusion.38
  207.2 7.1 %all-gather.1 = f32[32,4096]{1,0:T(8,128)S(1)} all-gather(f32[8,4096]{1,0:T(8,128)S(1)} %slice.9), channel_id=3, replica_groups=mesh['grp'=8,'slab'=4] {'slab'}, dimensions={0}, use_global_device_ids=true | all-gather | bytes 655360 | tf_op jit(solution)/shard_map/all_gather | solution.py:99
  214.4 1.3 fusion.15
  215.6 1.3 fusion.13
  216.9 2.0 fusion.35
  218.9 1.9 convolution_add_fusion.1
  220.8 3.2 %fusion = f32[1,128,4096]{2,1,0:T(8,128)} fusion(f32[128,4096]{1,0:T(8,128)S(1)} %convolution_add_fusion.1, f32[1,8,4096]{2,0,1:T(1,128)S(1)} %fusion.13, f32[128]{0:T(128)S(1)} %get-tuple-element.6, s32[128]{0:T(128)S(1)} %get-tuple-element.13), kind=kOutput, calls=%fused_computation.1 | convolution fusion | flops 50857984 | bytes 4326400 | tf_op jit(solution)/shard_map/dot_general | solution.py:43
  (28 shorter events, 0.5 us)
Async XLA Ops:
  6.5 188.7 %all-reduce.3.cloned.1.call-start = ((), (), s32[]{:S(2)}) async-start(), calls=%async_computation | async-start | bytes 8388608 | tf_op jit(solution)/shard_map/psum | solution.py:90
  21.0 10.9 %copy-start = (s32[1,128]{1,0:T(1,128)S(1)}, s32[1,128]{1,0:T(1,128)}, u32[]{:S(2)}) copy-start(s32[1,128]{1,0:T(1,128)} %param.7) | copy-start | bytes 1540
Sparse Core Ops, SparseCore 0:
  37.9 157.2 all-reduce.2
where the time goes:
time: 231 us
  waiting for transfers between devices  156 us (68%)
  matrix products  35.2 us (15%)
  blocking collectives  16 us (7%)
  between operations  15 us (6%)
  local copies, waits for them, and re-layouts  6.43 us (3%)
    psum x1, waiting for transfers between devices, shards(): total = lax.psum(term, 'grp')  156 us
    dot_general x8, matrix products, exact_dot(): jnp.dot(left, right, precision=lax.Precision.HIGHEST, preferred_element_t...  20.9 us
    all_gather x1, blocking collectives, shards(): planes = lax.all_gather(plane[None], 'slab', axis=0, tiled=True)  8.82 us
    all_gather x1, blocking collectives, shards(): top_planes = lax.all_gather(top_plane[None], 'slab', axis=0, tiled=True)  7.14 us
    dot_general x2, matrix products, inner_apply(): jnp.einsum('rjk,lk->rjl', shaped, rest_op, precision=lax.Precision.HIGHEST)  6.7 us
  transfers between devices with their start and end apart: 1, of which 1 were waited for; matrix products, arithmetic and copies ran while one was open for 1% of the time, Pallas kernels for 0%

commit v1 on v0

--- a/solution.py
+++ b/solution.py
@@ -87,7 +87,9 @@
     slot_ids = jnp.arange(per_slab, dtype=jnp.int32)
     gather_op = (slot_local[None, :] == slot_ids[:, None]).astype(jnp.float32)
     term = exact_dot(gather_op, scaled)
-    total = lax.psum(term, "grp")
+    total = term
+    for hop in (1, 2, 4):
+        total = total + lax.ppermute(total, "grp", [(dev, dev ^ hop) for dev in range(8)])
     spread_op = (slot_local[:, None] == slot_ids[None, :]).astype(jnp.float32)
     combined = exact_dot(spread_op, total)
     back_third = square_table(dehier_weight, P2)

time: 231 us -> 430 us (1.86)
  waiting for transfers between devices: 156 us -> 360 us
  between operations: 15 us -> 1.65 us
  starting transfers between devices: 0.01 us -> 5.82 us
    ppermute x0 -> x3, waiting for transfers between devices: none -> 360 us  [shards(): lax.ppermute(total, 'grp', [(dev, dev ^ hop) for dev in range(8)])]
    psum x1 -> x0, waiting for transfers between devices: 156 us -> none  [shards(): total = lax.psum(term, 'grp')]
    ppermute x0 -> x3, starting transfers between devices: none -> 5.82 us  [shards(): lax.ppermute(total, 'grp', [(dev, dev ^ hop) for dev in range(8)])]
  transfers between devices with their start and end apart: 1 -> 3, of which waited for: 1 -> 3; matrix products, arithmetic and copies ran while one was open for 1% -> 0% of each run, Pallas kernels for 0% -> 0%
where the time goes in v1:
time: 430 us; the launch traced here: 429 us
  waiting for transfers between devices  360 us (84%)
  matrix products  34.7 us (8%)
  blocking collectives  15.6 us (4%)
  local copies, waits for them, and re-layouts  6.43 us (1%)
  starting transfers between devices  5.82 us (1%)
  other arithmetic  5.15 us (1%)
    ppermute x3, waiting for transfers between devices, shards(): lax.ppermute(total, 'grp', [(dev, dev ^ hop) for dev in range(8)])  360 us
    dot_general x8, matrix products, exact_dot(): jnp.dot(left, right, precision=lax.Precision.HIGHEST, preferred_element_t...  20.4 us
    all_gather x1, blocking collectives, shards(): planes = lax.all_gather(plane[None], 'slab', axis=0, tiled=True)  8.83 us
  transfers between devices with their start and end apart: 3, of which 3 were waited for; matrix products, arithmetic and copies ran while one was open for 0% of the time, Pallas kernels for 0%

profile of v1, /device:TPU:0, one launch (start us, length us, event | category | flops | bytes accessed | tf_op | source)
XLA Modules:
  0.0 429.4 jit_solution(9592752023994268698)
XLA Ops:
  0.9 2.3 copy.16
  3.3 1.9 fusion.115
  5.2 1.5 broadcast_multiply_fusion.1
  6.7 2.4 reshape.448
  9.2 3.2 fusion.9
  12.4 2.0 fusion.40
  14.4 8.8 %all-gather = f32[32,4096]{1,0:T(8,128)S(1)} all-gather(f32[8,4096]{1,0:T(8,128)S(1)} %slice.8), channel_id=2, replica_groups=mesh['grp'=8,'slab'=4] {'slab'}, dimensions={0}, use_global_device_ids=true | all-gather | bytes 655360 | tf_op jit(solution)/shard_map/all_gather | solution.py:66
  25.3 2.1 fusion.1
  27.4 1.9 fusion.30
  29.3 1.6 collective-permute-start
  30.9 91.3 %collective-permute-done = f32[256,4096]{1,0:T(8,128)S(1)} collective-permute-done((f32[256,4096]{1,0:T(8,128)S(1)}, f32[256,4096]{1,0:T(8,128)S(1)}, u32[]{:S(2)}, u32[]{:S(2)}) %collective-permute-start) | collective-permute-done | bytes 4194336 | tf_op jit(solution)/shard_map/ppermute | solution.py:92
  122.9 1.6 collective-permute-start.1
  124.5 90.4 %collective-permute-done.1 = f32[256,4096]{1,0:T(8,128)S(1)} collective-permute-done((f32[256,4096]{1,0:T(8,128)S(1)}, f32[256,4096]{1,0:T(8,128)S(1)}, u32[]{:S(2)}, u32[]{:S(2)}) %collective-permute-start.1) | collective-permute-done | bytes 4194336 | tf_op jit(solution)/shard_map/ppermute | solution.py:92
  214.9 2.5 add.146
  217.4 2.6 collective-permute-start.2
  221.2 178.4 %collective-permute-done.2 = f32[256,4096]{1,0:T(8,128)} collective-permute-done((f32[256,4096]{1,0:T(8,128)}, f32[256,4096]{1,0:T(8,128)}, u32[]{:S(2)}, u32[]{:S(2)}) %collective-permute-start.2) | collective-permute-done | bytes 4194336 | tf_op jit(solution)/shard_map/ppermute | solution.py:92
  399.6 5.3 %fusion.2 = f32[128,4096]{1,0:T(8,128)S(1)} fusion(f32[256,4096]{1,0:T(8,128)} %add.146, f32[256,4096]{1,0:T(8,128)} %collective-permute-done.2, s32[128]{0:T(128)S(1)} %and_select_fusion.3), kind=kOutput, calls=%fused_computation.5 | convolution fusion | flops 1611694080 | bytes 10486272 | tf_op jit(solution)/shard_map/dot_general | solution.py:43
  405.6 2.2 fusion.113
  407.7 3.2 fusion.7
  411.0 2.0 fusion.39
  413.0 6.8 %all-gather.1 = f32[32,4096]{1,0:T(8,128)S(1)} all-gather(f32[8,4096]{1,0:T(8,128)S(1)} %slice.9), channel_id=3, replica_groups=mesh['grp'=8,'slab'=4] {'slab'}, dimensions={0}, use_global_device_ids=true | all-gather | bytes 655360 | tf_op jit(solution)/shard_map/all_gather | solution.py:101
  422.3 2.0 fusion.36
  424.3 1.9 convolution_add_fusion.1
  426.2 3.2 fusion
  (33 shorter events, 6.6 us)
Async XLA Ops:
  14.4 10.9 %copy-start = (s32[1,128]{1,0:T(1,128)S(1)}, s32[1,128]{1,0:T(1,128)}, u32[]{:S(2)}) copy-start(s32[1,128]{1,0:T(1,128)} %param.7) | copy-start | bytes 1540
  29.3 92.9 %collective-permute-start = (f32[256,4096]{1,0:T(8,128)S(1)}, f32[256,4096]{1,0:T(8,128)S(1)}, u32[]{:S(2)}, u32[]{:S(2)}) collective-permute-start(f32[256,4096]{1,0:T(8,128)S(1)} %fusion.30), channel_id=1, source_target_pairs={{0,4},{4,0},{8,12},{12,8},{16,20},{20,16},{24,28},{28,24},{1,5},{5... | collective-permute-start | bytes 12582920 | tf_op jit(solution)/shard_map/ppermute | solution.py:92
  122.9 92.0 %collective-permute-start.1 = (f32[256,4096]{1,0:T(8,128)S(1)}, f32[256,4096]{1,0:T(8,128)S(1)}, u32[]{:S(2)}, u32[]{:S(2)}) collective-permute-start(f32[256,4096]{1,0:T(8,128)S(1)} %add.145), channel_id=1, source_target_pairs={{0,8},{4,12},{8,0},{12,4},{16,24},{20,28},{24,16},{28,20},{1,9},{5... | collective-permute-start | bytes 12582920 | tf_op jit(solution)/shard_map/ppermute | solution.py:92
  217.4 182.2 %collective-permute-start.2 = (f32[256,4096]{1,0:T(8,128)}, f32[256,4096]{1,0:T(8,128)}, u32[]{:S(2)}, u32[]{:S(2)}) collective-permute-start(f32[256,4096]{1,0:T(8,128)} %add.146), channel_id=1, source_target_pairs={{0,16},{4,20},{8,24},{12,28},{16,0},{20,4},{24,8},{28,12},{1,17},{... | collective-permute-start | bytes 12582920 | tf_op jit(solution)/shard_map/ppermute | solution.py:92
